TPU v7x, 32 devices: a whole 2x2x4 slice. The times are simulated.
32 devices in a mesh: row: 4 (over y, x), col: 8 (over z, core).
Axes of the slice: x: 2, y: 2, z: 4, core: 2. Of those that a mesh axis runs over, the one named last changes fastest.
Arguments:
- matrix: float32 [2, 4, 256, 1, 8, 256], P(None, 'row', None, None, 'col'), as said below
Outputs:
- factored: float32 [2, 4, 256, 1, 8, 256], P(None, 'row', None, None, 'col')
Inputs may be any that keep to these rules, and one draw needn't show every extreme that they name: `matrix`: symmetric and positive definite.
All inputs are finite; a program needn't handle non-finite values.
Results may differ from a plain program's by a relative error of at most 0.0001.
Values sent between devices are 32-bit elements; how exact they have to be, the bound alone decides.
A program may use at most 128 MiB of HBM per device.

v0:
```python
import jax
import jax.numpy as jnp
from jax import lax
from jax.sharding import PartitionSpec as P

STEPS = 8


def broadcast(value, axis, source):
    kept = jnp.where(lax.axis_index(axis) == source, value, 0).astype(value.dtype)
    return lax.psum(kept, axis)


def solve_panel(factor, column):
    width = column.shape[1]
    inverse = jax.scipy.linalg.solve_triangular(
        factor, jnp.eye(width, dtype=jnp.float32), lower=True
    )
    solved = jnp.einsum("ts,ars->art", inverse, column, precision=lax.Precision.HIGHEST)
    return solved


def on_device(matrix):
    row_tiles = matrix.shape[0]
    width = matrix.shape[2]
    col_tiles = matrix.shape[3]
    tile_grid = matrix.reshape(row_tiles, width, col_tiles, width)
    num_row = lax.axis_size("row")
    num_col = lax.axis_size("col")
    my_row = lax.axis_index("row")
    my_col = lax.axis_index("col")
    rows_global = jnp.arange(row_tiles, dtype=jnp.int32) * num_row + my_row
    ratio = num_col // num_row
    for k in range(STEPS):
        lead_row = k % num_row
        lead_col = k % num_col
        local_row = k // num_row
        local_col = k // num_col
        column = tile_grid[:, :, local_col, :]
        candidate = tile_grid[local_row, :, local_col, :]
        keep = (rows_global > k)[:, None, None]
        diag_tile = broadcast(candidate, "row", lead_row)
        factor = jnp.linalg.cholesky(diag_tile)
        local_panel = jnp.where(keep, solve_panel(factor, column), 0.0)
        panel_rows = broadcast(local_panel, "col", lead_col)
        grouped = panel_rows.reshape(col_tiles, ratio, width, width)
        chosen = lax.dynamic_index_in_dim(grouped, my_col // num_row, 1, keepdims=False)
        panel_cols = broadcast(chosen, "row", my_col % num_row)
        update = jnp.einsum(
            "art,bst->arbs", panel_rows, panel_cols, precision=lax.Precision.HIGHEST
        )
        tile_grid = tile_grid - update
        diagonal_part = jnp.where((rows_global == k)[:, None, None], factor[None], 0.0)
        new_column = panel_rows + diagonal_part
        old_column = tile_grid[:, :, local_col, :]
        tile_grid = tile_grid.at[:, :, local_col, :].set(
            jnp.where(my_col == lead_col, new_column, old_column)
        )
    return tile_grid.reshape(matrix.shape)


def solution(mesh):
    placed = (P(None, "row", None, None, "col", None),)
    return jax.shard_map(
        on_device,
        mesh=mesh,
        in_specs=placed,
        out_specs=P(None, "row", None, None, "col", None),
        check_vma=False,
    )
```

profile of v0, /device:TPU:0, one launch (start us, length us, event | category | flops | bytes accessed | tf_op | source)
XLA Modules:
  0.0 1724.1 jit_solution(9675084317404435007)
XLA Ops:
  9.2 46.9 %all-reduce.26.cloned.1.call-done = f32[256,256]{0,1:T(8,128)} async-done(((f32[256,256]{0,1:T(8,128)}), f32[256,256]{0,1:T(8,128)}) %all-reduce.26.cloned.1.call-update) | async-done | bytes 262160 | tf_op jit(solution)/shard_map/psum | solution.py:11
  119.8 56.6 %all-reduce.28.cloned.1.call-done = f32[2,256,256]{1,2,0:T(8,128)} async-done(((f32[2,256,256]{1,2,0:T(8,128)}), f32[2,256,256]{1,2,0:T(8,128)}) %all-reduce.28.cloned.1.call-update) | async-done | bytes 524304 | tf_op jit(solution)/shard_map/psum | solution.py:11
  178.6 42.8 %all-reduce.30.cloned.1.call-done = f32[256,256]{0,1:T(8,128)} async-done(((f32[256,256]{0,1:T(8,128)}), f32[256,256]{0,1:T(8,128)}) %all-reduce.30.cloned.1.call-update) | async-done | bytes 262160 | tf_op jit(solution)/shard_map/psum | solution.py:11
  223.9 43.4 %all-reduce.32.cloned.1.call-done = f32[256,256]{0,1:T(8,128)} async-done(((f32[256,256]{0,1:T(8,128)}), f32[256,256]{0,1:T(8,128)}) %all-reduce.32.cloned.1.call-update) | async-done | bytes 262160 | tf_op jit(solution)/shard_map/psum | solution.py:11
  341.8 56.6 %all-reduce.34.cloned.1.call-done = f32[2,256,256]{1,2,0:T(8,128)} async-done(((f32[2,256,256]{1,2,0:T(8,128)}), f32[2,256,256]{1,2,0:T(8,128)}) %all-reduce.34.cloned.1.call-update) | async-done | bytes 524304 | tf_op jit(solution)/shard_map/psum | solution.py:11
  400.3 43.0 %all-reduce.36.cloned.1.call-done = f32[256,256]{0,1:T(8,128)} async-done(((f32[256,256]{0,1:T(8,128)}), f32[256,256]{0,1:T(8,128)}) %all-reduce.36.cloned.1.call-update) | async-done | bytes 262160 | tf_op jit(solution)/shard_map/psum | solution.py:11
  445.8 43.5 %all-reduce.38.cloned.1.call-done = f32[256,256]{0,1:T(8,128)} async-done(((f32[256,256]{0,1:T(8,128)}), f32[256,256]{0,1:T(8,128)}) %all-reduce.38.cloned.1.call-update) | async-done | bytes 262160 | tf_op jit(solution)/shard_map/psum | solution.py:11
  553.8 56.6 %all-reduce.40.cloned.1.call-done = f32[2,256,256]{1,2,0:T(8,128)} async-done(((f32[2,256,256]{1,2,0:T(8,128)}), f32[2,256,256]{1,2,0:T(8,128)}) %all-reduce.40.cloned.1.call-update) | async-done | bytes 524304 | tf_op jit(solution)/shard_map/psum | solution.py:11
  612.3 43.2 %all-reduce.42.cloned.1.call-done = f32[256,256]{0,1:T(8,128)} async-done(((f32[256,256]{0,1:T(8,128)}), f32[256,256]{0,1:T(8,128)}) %all-reduce.42.cloned.1.call-update) | async-done | bytes 262160 | tf_op jit(solution)/shard_map/psum | solution.py:11
  657.9 43.4 %all-reduce.44.cloned.1.call-done = f32[256,256]{0,1:T(8,128)} async-done(((f32[256,256]{0,1:T(8,128)}), f32[256,256]{0,1:T(8,128)}) %all-reduce.44.cloned.1.call-update) | async-done | bytes 262160 | tf_op jit(solution)/shard_map/psum | solution.py:11
  765.5 56.6 %all-reduce.46.cloned.1.call-done = f32[2,256,256]{1,2,0:T(8,128)} async-done(((f32[2,256,256]{1,2,0:T(8,128)}), f32[2,256,256]{1,2,0:T(8,128)}) %all-reduce.46.cloned.1.call-update) | async-done | bytes 524304 | tf_op jit(solution)/shard_map/psum | solution.py:11
  824.0 43.0 %all-reduce.48.cloned.1.call-done = f32[256,256]{0,1:T(8,128)} async-done(((f32[256,256]{0,1:T(8,128)}), f32[256,256]{0,1:T(8,128)}) %all-reduce.48.cloned.1.call-update) | async-done | bytes 262160 | tf_op jit(solution)/shard_map/psum | solution.py:11
  869.5 43.5 %all-reduce.50.cloned.1.call-done = f32[256,256]{0,1:T(8,128)} async-done(((f32[256,256]{0,1:T(8,128)}), f32[256,256]{0,1:T(8,128)}) %all-reduce.50.cloned.1.call-update) | async-done | bytes 262160 | tf_op jit(solution)/shard_map/psum | solution.py:11
  977.4 56.7 %all-reduce.52.cloned.1.call-done = f32[2,256,256]{1,2,0:T(8,128)} async-done(((f32[2,256,256]{1,2,0:T(8,128)}), f32[2,256,256]{1,2,0:T(8,128)}) %all-reduce.52.cloned.1.call-update) | async-done | bytes 524304 | tf_op jit(solution)/shard_map/psum | solution.py:11
  1036.0 43.0 %all-reduce.54.cloned.1.call-done = f32[256,256]{0,1:T(8,128)} async-done(((f32[256,256]{0,1:T(8,128)}), f32[256,256]{0,1:T(8,128)}) %all-reduce.54.cloned.1.call-update) | async-done | bytes 262160 | tf_op jit(solution)/shard_map/psum | solution.py:11
  1081.4 43.4 %all-reduce.56.cloned.1.call-done = f32[256,256]{0,1:T(8,128)} async-done(((f32[256,256]{0,1:T(8,128)}), f32[256,256]{0,1:T(8,128)}) %all-reduce.56.cloned.1.call-update) | async-done | bytes 262160 | tf_op jit(solution)/shard_map/psum | solution.py:11
  1189.0 56.6 %all-reduce.58.cloned.1.call-done = f32[2,256,256]{1,2,0:T(8,128)} async-done(((f32[2,256,256]{1,2,0:T(8,128)}), f32[2,256,256]{1,2,0:T(8,128)}) %all-reduce.58.cloned.1.call-update) | async-done | bytes 524304 | tf_op jit(solution)/shard_map/psum | solution.py:11
  1247.5 43.0 %all-reduce.60.cloned.1.call-done = f32[256,256]{0,1:T(8,128)} async-done(((f32[256,256]{0,1:T(8,128)}), f32[256,256]{0,1:T(8,128)}) %all-reduce.60.cloned.1.call-update) | async-done | bytes 262160 | tf_op jit(solution)/shard_map/psum | solution.py:11
  1293.0 43.5 %all-reduce.62.cloned.1.call-done = f32[256,256]{0,1:T(8,128)} async-done(((f32[256,256]{0,1:T(8,128)}), f32[256,256]{0,1:T(8,128)}) %all-reduce.62.cloned.1.call-update) | async-done | bytes 262160 | tf_op jit(solution)/shard_map/psum | solution.py:11
  1400.7 56.6 %all-reduce.64.cloned.1.call-done = f32[2,256,256]{1,2,0:T(8,128)} async-done(((f32[2,256,256]{1,2,0:T(8,128)}), f32[2,256,256]{1,2,0:T(8,128)}) %all-reduce.64.cloned.1.call-update) | async-done | bytes 524304 | tf_op jit(solution)/shard_map/psum | solution.py:11
  1459.2 43.2 %all-reduce.66.cloned.1.call-done = f32[256,256]{0,1:T(8,128)} async-done(((f32[256,256]{0,1:T(8,128)}), f32[256,256]{0,1:T(8,128)}) %all-reduce.66.cloned.1.call-update) | async-done | bytes 262160 | tf_op jit(solution)/shard_map/psum | solution.py:11
  1504.9 43.5 %all-reduce.68.cloned.1.call-done = f32[256,256]{0,1:T(8,128)} async-done(((f32[256,256]{0,1:T(8,128)}), f32[256,256]{0,1:T(8,128)}) %all-reduce.68.cloned.1.call-update) | async-done | bytes 262160 | tf_op jit(solution)/shard_map/psum | solution.py:11
  1612.6 56.6 %all-reduce.70.cloned.1.call-done = f32[2,256,256]{1,2,0:T(8,128)} async-done(((f32[2,256,256]{1,2,0:T(8,128)}), f32[2,256,256]{1,2,0:T(8,128)}) %all-reduce.70.cloned.1.call-update) | async-done | bytes 524304 | tf_op jit(solution)/shard_map/psum | solution.py:11
  1671.1 43.1 %all-reduce.72.cloned.1.call-done = f32[256,256]{0,1:T(8,128)} async-done(((f32[256,256]{0,1:T(8,128)}), f32[256,256]{0,1:T(8,128)}) %all-reduce.72.cloned.1.call-update) | async-done | bytes 262160 | tf_op jit(solution)/shard_map/psum | solution.py:11
  (354 shorter events, 582.3 us)
Async XLA Ops:
  6.5 49.5 %all-reduce.26.cloned.1.call-start = ((), (), s32[]{:S(2)}) async-start(), calls=%async_computation | async-start | bytes 524288 | tf_op jit(solution)/shard_map/psum | solution.py:11
  8.4 167.9 %all-reduce.28.cloned.1.call-start = ((), (), s32[]{:S(2)}) async-start(), calls=%async_computation.1 | async-start | bytes 1048576 | tf_op jit(solution)/shard_map/psum | solution.py:11
  119.7 101.7 %all-reduce.30.cloned.1.call-start = ((), (), s32[]{:S(2)}) async-start(), calls=%async_computation.2 | async-start | bytes 524288 | tf_op jit(solution)/shard_map/psum | solution.py:11
  178.0 89.2 %all-reduce.32.cloned.1.call-start = ((), (), s32[]{:S(2)}) async-start(), calls=%async_computation.3 | async-start | bytes 524288 | tf_op jit(solution)/shard_map/psum | solution.py:11
  223.8 174.6 %all-reduce.34.cloned.1.call-start = ((), (), s32[]{:S(2)}) async-start(), calls=%async_computation.4 | async-start | bytes 1048576 | tf_op jit(solution)/shard_map/psum | solution.py:11
  341.8 101.6 %all-reduce.36.cloned.1.call-start = ((), (), s32[]{:S(2)}) async-start(), calls=%async_computation.5 | async-start | bytes 524288 | tf_op jit(solution)/shard_map/psum | solution.py:11
  400.1 89.2 %all-reduce.38.cloned.1.call-start = ((), (), s32[]{:S(2)}) async-start(), calls=%async_computation.6 | async-start | bytes 524288 | tf_op jit(solution)/shard_map/psum | solution.py:11
  445.8 164.6 %all-reduce.40.cloned.1.call-start = ((), (), s32[]{:S(2)}) async-start(), calls=%async_computation.7 | async-start | bytes 1048576 | tf_op jit(solution)/shard_map/psum | solution.py:11
  553.7 101.8 %all-reduce.42.cloned.1.call-start = ((), (), s32[]{:S(2)}) async-start(), calls=%async_computation.8 | async-start | bytes 524288 | tf_op jit(solution)/shard_map/psum | solution.py:11
  612.1 89.2 %all-reduce.44.cloned.1.call-start = ((), (), s32[]{:S(2)}) async-start(), calls=%async_computation.9 | async-start | bytes 524288 | tf_op jit(solution)/shard_map/psum | solution.py:11
  657.9 164.2 %all-reduce.46.cloned.1.call-start = ((), (), s32[]{:S(2)}) async-start(), calls=%async_computation.10 | async-start | bytes 1048576 | tf_op jit(solution)/shard_map/psum | solution.py:11
  765.5 101.6 %all-reduce.48.cloned.1.call-start = ((), (), s32[]{:S(2)}) async-start(), calls=%async_computation.11 | async-start | bytes 524288 | tf_op jit(solution)/shard_map/psum | solution.py:11
  823.8 89.2 %all-reduce.50.cloned.1.call-start = ((), (), s32[]{:S(2)}) async-start(), calls=%async_computation.12 | async-start | bytes 524288 | tf_op jit(solution)/shard_map/psum | solution.py:11
  869.4 164.6 %all-reduce.52.cloned.1.call-start = ((), (), s32[]{:S(2)}) async-start(), calls=%async_computation.13 | async-start | bytes 1048576 | tf_op jit(solution)/shard_map/psum | solution.py:11
  977.4 101.6 %all-reduce.54.cloned.1.call-start = ((), (), s32[]{:S(2)}) async-start(), calls=%async_computation.14 | async-start | bytes 524288 | tf_op jit(solution)/shard_map/psum | solution.py:11
  1035.8 89.0 %all-reduce.56.cloned.1.call-start = ((), (), s32[]{:S(2)}) async-start(), calls=%async_computation.15 | async-start | bytes 524288 | tf_op jit(solution)/shard_map/psum | solution.py:11
  1081.4 164.2 %all-reduce.58.cloned.1.call-start = ((), (), s32[]{:S(2)}) async-start(), calls=%async_computation.16 | async-start | bytes 1048576 | tf_op jit(solution)/shard_map/psum | solution.py:11
  1188.9 101.6 %all-reduce.60.cloned.1.call-start = ((), (), s32[]{:S(2)}) async-start(), calls=%async_computation.17 | async-start | bytes 524288 | tf_op jit(solution)/shard_map/psum | solution.py:11
  1247.3 89.2 %all-reduce.62.cloned.1.call-start = ((), (), s32[]{:S(2)}) async-start(), calls=%async_computation.18 | async-start | bytes 524288 | tf_op jit(solution)/shard_map/psum | solution.py:11
  1292.9 164.4 %all-reduce.64.cloned.1.call-start = ((), (), s32[]{:S(2)}) async-start(), calls=%async_computation.19 | async-start | bytes 1048576 | tf_op jit(solution)/shard_map/psum | solution.py:11
  1400.7 101.7 %all-reduce.66.cloned.1.call-start = ((), (), s32[]{:S(2)}) async-start(), calls=%async_computation.20 | async-start | bytes 524288 | tf_op jit(solution)/shard_map/psum | solution.py:11
  1459.0 89.3 %all-reduce.68.cloned.1.call-start = ((), (), s32[]{:S(2)}) async-start(), calls=%async_computation.21 | async-start | bytes 524288 | tf_op jit(solution)/shard_map/psum | solution.py:11
  1504.8 164.4 %all-reduce.70.cloned.1.call-start = ((), (), s32[]{:S(2)}) async-start(), calls=%async_computation.22 | async-start | bytes 1048576 | tf_op jit(solution)/shard_map/psum | solution.py:11
  1612.6 101.5 %all-reduce.72.cloned.1.call-start = ((), (), s32[]{:S(2)}) async-start(), calls=%async_computation.23 | async-start | bytes 524288 | tf_op jit(solution)/shard_map/psum | solution.py:11
  (18 other events, 357.3 us)
Sparse Core Ops, SparseCore 0:
  10.3 45.7 all-reduce.25
  119.8 56.4 all-reduce.27
  179.3 42.0 all-reduce.29
  224.2 43.0 all-reduce.31
  341.9 56.4 all-reduce.33
  401.2 42.0 all-reduce.35
  446.3 43.0 all-reduce.37
  553.8 56.5 all-reduce.39
  613.3 42.0 all-reduce.41
  658.2 43.0 all-reduce.43
  765.6 56.4 all-reduce.45
  824.9 42.0 all-reduce.47
  869.9 43.0 all-reduce.49
  977.5 56.5 all-reduce.51
  1036.8 42.0 all-reduce.53
  1081.7 43.0 all-reduce.55
  1189.1 56.4 all-reduce.57
  1248.4 42.0 all-reduce.59
  1293.4 43.0 all-reduce.61
  1400.8 56.5 all-reduce.63
  1460.2 42.0 all-reduce.65
  1505.3 43.0 all-reduce.67
  1612.7 56.4 all-reduce.69
  1672.0 42.0 all-reduce.71
where the time goes:
time: 1730 us; the launch traced here: 1720 us
  waiting for transfers between devices  1150 us (66%)
  other arithmetic  454 us (26%)
  local copies, waits for them, and re-layouts  46.2 us (3%)
  matrix products  35.5 us (2%)
  between operations  26.2 us (2%)
    psum x24, waiting for transfers between devices, broadcast(): return lax.psum(kept, axis)  1150 us
    another operation x55, other arithmetic, on_device(): factor = jnp.linalg.cholesky(diag_tile)  277 us
    another operation x17, other arithmetic, solve_panel(): jax.scipy.linalg.solve_triangular(factor, jnp.eye(width, dtype=jnp.float3...  158 us
  transfers between devices with their start and end apart: 24, of which 24 were waited for; matrix products, arithmetic and copies ran while one was open for 0% of the time, Pallas kernels for 0%

commit v1 on v0

--- a/solution.py
+++ b/solution.py
@@ -8,7 +8,7 @@
 
 def broadcast(value, axis, source):
     kept = jnp.where(lax.axis_index(axis) == source, value, 0).astype(value.dtype)
-    return lax.psum(kept, axis)
+    return lax.all_gather(kept, axis_name=axis).sum(axis=0)
 
 
 def solve_panel(factor, column):

time: 1730 us -> 1400 us (0.81)
  waiting for transfers between devices: 1150 us -> 795 us
  other arithmetic: 454 us -> 488 us
    psum x24 -> x0, waiting for transfers between devices: 1150 us -> none  [broadcast(): return lax.psum(kept, axis)]
    all_gather x0 -> x24, waiting for transfers between devices: none -> 795 us  [broadcast(): return lax.all_gather(kept, axis_name=axis).sum(axis=0)]
    reduce_sum x0 -> x23, other arithmetic: none -> 38.7 us  [broadcast(): return lax.all_gather(kept, axis_name=axis).sum(axis=0)]
where the time goes in v1:
time: 1400 us; the launch traced here: 1390 us
  waiting for transfers between devices  795 us (57%)
  other arithmetic  488 us (35%)
  local copies, waits for them, and re-layouts  37.4 us (3%)
  matrix products  26.3 us (2%)
  between operations  26.1 us (2%)
    all_gather x24, waiting for transfers between devices, broadcast(): return lax.all_gather(kept, axis_name=axis).sum(axis=0)  795 us
    another operation x55, other arithmetic, on_device(): factor = jnp.linalg.cholesky(diag_tile)  277 us
    another operation x17, other arithmetic, solve_panel(): jax.scipy.linalg.solve_triangular(factor, jnp.eye(width, dtype=jnp.float3...  158 us
    reduce_sum x23, other arithmetic, broadcast(): return lax.all_gather(kept, axis_name=axis).sum(axis=0)  38.7 us
    another operation x57, local copies, waits for them, and re-layouts, solve_panel(): jax.scipy.linalg.solve_triangular(factor, jnp.eye(width, dtype=jnp.float3...  32.6 us
  transfers between devices with their start and end apart: 24, of which 24 were waited for; matrix products, arithmetic and copies ran while one was open for 0% of the time, Pallas kernels for 0%

profile of v1, /device:TPU:0, one launch (start us, length us, event | category | flops | bytes accessed | tf_op | source)
XLA Modules:
  0.0 1386.7 jit_solution(12965815197017878945)
XLA Ops:
  8.6 29.8 %all-gather.56.cloned.1.call-done = f32[4,1,256,1,1,256]{5,2,4,3,1,0:T(8,128)} async-done(((f32[1,1,256,1,1,256]{5,2,4,3,1,0:T(8,128)}), f32[4,1,256,1,1,256]{5,2,4,3,1,0:T(8,128)}) %all-gather.56.cloned.1.call-update) | async-done | bytes 1048592 | tf_op jit(solution)/shard_map/all_gather | solution.py:11
  102.7 46.9 %all-gather.58.cloned.1.call-done = f32[16,256,256]{2,1,0:T(8,128)} async-done(((f32[2,256,256]{2,1,0:T(8,128)}), f32[16,256,256]{2,1,0:T(8,128)}) %all-gather.58.cloned.1.call-update) | async-done | bytes 4194320 | tf_op jit(solution)/shard_map/all_gather | solution.py:11
  153.0 25.4 %all-gather.60.cloned.1.call-done = f32[4,256,256]{2,1,0:T(8,128)} async-done(((f32[1,256,256]{2,1,0:T(8,128)}), f32[4,256,256]{2,1,0:T(8,128)}) %all-gather.60.cloned.1.call-update) | async-done | bytes 1048592 | tf_op jit(solution)/shard_map/all_gather | solution.py:11
  181.1 26.6 %all-gather.42.cloned.1.call-done = f32[4,256,256]{2,1,0:T(8,128)} async-done(((f32[1,256,256]{2,1,0:T(8,128)}), f32[4,256,256]{2,1,0:T(8,128)}) %all-gather.42.cloned.1.call-update) | async-done | bytes 1048592 | tf_op jit(solution)/shard_map/all_gather | solution.py:11
  282.8 47.0 %all-gather.62.cloned.1.call-done = f32[16,256,256]{2,1,0:T(8,128)} async-done(((f32[2,256,256]{2,1,0:T(8,128)}), f32[16,256,256]{2,1,0:T(8,128)}) %all-gather.62.cloned.1.call-update) | async-done | bytes 4194320 | tf_op jit(solution)/shard_map/all_gather | solution.py:11
  333.1 25.4 %all-gather.64.cloned.1.call-done = f32[4,256,256]{2,1,0:T(8,128)} async-done(((f32[1,256,256]{2,1,0:T(8,128)}), f32[4,256,256]{2,1,0:T(8,128)}) %all-gather.64.cloned.1.call-update) | async-done | bytes 1048592 | tf_op jit(solution)/shard_map/all_gather | solution.py:11
  361.3 26.6 %all-gather.44.cloned.1.call-done = f32[4,256,256]{2,1,0:T(8,128)} async-done(((f32[1,256,256]{2,1,0:T(8,128)}), f32[4,256,256]{2,1,0:T(8,128)}) %all-gather.44.cloned.1.call-update) | async-done | bytes 1048592 | tf_op jit(solution)/shard_map/all_gather | solution.py:11
  452.5 47.0 %all-gather.66.cloned.1.call-done = f32[16,256,256]{2,1,0:T(8,128)} async-done(((f32[2,256,256]{2,1,0:T(8,128)}), f32[16,256,256]{2,1,0:T(8,128)}) %all-gather.66.cloned.1.call-update) | async-done | bytes 4194320 | tf_op jit(solution)/shard_map/all_gather | solution.py:11
  502.8 25.4 %all-gather.68.cloned.1.call-done = f32[4,256,256]{2,1,0:T(8,128)} async-done(((f32[1,256,256]{2,1,0:T(8,128)}), f32[4,256,256]{2,1,0:T(8,128)}) %all-gather.68.cloned.1.call-update) | async-done | bytes 1048592 | tf_op jit(solution)/shard_map/all_gather | solution.py:11
  531.0 26.6 %all-gather.46.cloned.1.call-done = f32[4,256,256]{2,1,0:T(8,128)} async-done(((f32[1,256,256]{2,1,0:T(8,128)}), f32[4,256,256]{2,1,0:T(8,128)}) %all-gather.46.cloned.1.call-update) | async-done | bytes 1048592 | tf_op jit(solution)/shard_map/all_gather | solution.py:11
  622.0 47.0 %all-gather.70.cloned.1.call-done = f32[16,256,256]{2,1,0:T(8,128)} async-done(((f32[2,256,256]{2,1,0:T(8,128)}), f32[16,256,256]{2,1,0:T(8,128)}) %all-gather.70.cloned.1.call-update) | async-done | bytes 4194320 | tf_op jit(solution)/shard_map/all_gather | solution.py:11
  672.4 25.4 %all-gather.72.cloned.1.call-done = f32[4,256,256]{2,1,0:T(8,128)} async-done(((f32[1,256,256]{2,1,0:T(8,128)}), f32[4,256,256]{2,1,0:T(8,128)}) %all-gather.72.cloned.1.call-update) | async-done | bytes 1048592 | tf_op jit(solution)/shard_map/all_gather | solution.py:11
  700.5 26.6 %all-gather.48.cloned.1.call-done = f32[4,256,256]{2,1,0:T(8,128)} async-done(((f32[1,256,256]{2,1,0:T(8,128)}), f32[4,256,256]{2,1,0:T(8,128)}) %all-gather.48.cloned.1.call-update) | async-done | bytes 1048592 | tf_op jit(solution)/shard_map/all_gather | solution.py:11
  791.8 47.0 %all-gather.74.cloned.1.call-done = f32[16,256,256]{2,1,0:T(8,128)} async-done(((f32[2,256,256]{2,1,0:T(8,128)}), f32[16,256,256]{2,1,0:T(8,128)}) %all-gather.74.cloned.1.call-update) | async-done | bytes 4194320 | tf_op jit(solution)/shard_map/all_gather | solution.py:11
  842.1 25.4 %all-gather.76.cloned.1.call-done = f32[4,256,256]{2,1,0:T(8,128)} async-done(((f32[1,256,256]{2,1,0:T(8,128)}), f32[4,256,256]{2,1,0:T(8,128)}) %all-gather.76.cloned.1.call-update) | async-done | bytes 1048592 | tf_op jit(solution)/shard_map/all_gather | solution.py:11
  870.3 26.6 %all-gather.50.cloned.1.call-done = f32[4,256,256]{2,1,0:T(8,128)} async-done(((f32[1,256,256]{2,1,0:T(8,128)}), f32[4,256,256]{2,1,0:T(8,128)}) %all-gather.50.cloned.1.call-update) | async-done | bytes 1048592 | tf_op jit(solution)/shard_map/all_gather | solution.py:11
  961.3 47.0 %all-gather.78.cloned.1.call-done = f32[16,256,256]{2,1,0:T(8,128)} async-done(((f32[2,256,256]{2,1,0:T(8,128)}), f32[16,256,256]{2,1,0:T(8,128)}) %all-gather.78.cloned.1.call-update) | async-done | bytes 4194320 | tf_op jit(solution)/shard_map/all_gather | solution.py:11
  1011.6 25.4 %all-gather.80.cloned.1.call-done = f32[4,256,256]{2,1,0:T(8,128)} async-done(((f32[1,256,256]{2,1,0:T(8,128)}), f32[4,256,256]{2,1,0:T(8,128)}) %all-gather.80.cloned.1.call-update) | async-done | bytes 1048592 | tf_op jit(solution)/shard_map/all_gather | solution.py:11
  1039.8 26.6 %all-gather.52.cloned.1.call-done = f32[4,256,256]{2,1,0:T(8,128)} async-done(((f32[1,256,256]{2,1,0:T(8,128)}), f32[4,256,256]{2,1,0:T(8,128)}) %all-gather.52.cloned.1.call-update) | async-done | bytes 1048592 | tf_op jit(solution)/shard_map/all_gather | solution.py:11
  1130.9 47.0 %all-gather.82.cloned.1.call-done = f32[16,256,256]{2,1,0:T(8,128)} async-done(((f32[2,256,256]{2,1,0:T(8,128)}), f32[16,256,256]{2,1,0:T(8,128)}) %all-gather.82.cloned.1.call-update) | async-done | bytes 4194320 | tf_op jit(solution)/shard_map/all_gather | solution.py:11
  1181.2 25.4 %all-gather.84.cloned.1.call-done = f32[4,256,256]{2,1,0:T(8,128)} async-done(((f32[1,256,256]{2,1,0:T(8,128)}), f32[4,256,256]{2,1,0:T(8,128)}) %all-gather.84.cloned.1.call-update) | async-done | bytes 1048592 | tf_op jit(solution)/shard_map/all_gather | solution.py:11
  1209.3 26.6 %all-gather.54.cloned.1.call-done = f32[4,256,256]{2,1,0:T(8,128)} async-done(((f32[1,256,256]{2,1,0:T(8,128)}), f32[4,256,256]{2,1,0:T(8,128)}) %all-gather.54.cloned.1.call-update) | async-done | bytes 1048592 | tf_op jit(solution)/shard_map/all_gather | solution.py:11
  1300.5 47.0 %all-gather.86.cloned.1.call-done = f32[16,256,256]{2,1,0:T(8,128)} async-done(((f32[2,256,256]{2,1,0:T(8,128)}), f32[16,256,256]{2,1,0:T(8,128)}) %all-gather.86.cloned.1.call-update) | async-done | bytes 4194320 | tf_op jit(solution)/shard_map/all_gather | solution.py:11
  1350.7 25.4 %all-gather.88.cloned.1.call-done = f32[4,256,256]{2,1,0:T(8,128)} async-done(((f32[1,256,256]{2,1,0:T(8,128)}), f32[4,256,256]{2,1,0:T(8,128)}) %all-gather.88.cloned.1.call-update) | async-done | bytes 1048592 | tf_op jit(solution)/shard_map/all_gather | solution.py:11
  (335 shorter events, 598.3 us)
Async XLA Ops:
  6.5 31.9 %all-gather.56.cloned.1.call-start = ((), (), s32[]{:S(2)}) async-start(), calls=%async_computation.7 | async-start | bytes 1310720 | tf_op jit(solution)/shard_map/all_gather | solution.py:11
  8.5 141.1 %all-gather.58.cloned.1.call-start = ((), (), s32[]{:S(2)}) async-start(), calls=%async_computation.8 | async-start | bytes 4718592 | tf_op jit(solution)/shard_map/all_gather | solution.py:11
  102.6 75.7 %all-gather.60.cloned.1.call-start = ((), (), s32[]{:S(2)}) async-start(), calls=%async_computation.9 | async-start | bytes 1310720 | tf_op jit(solution)/shard_map/all_gather | solution.py:11
  152.9 54.8 %all-gather.42.cloned.1.call-start = ((), (), s32[]{:S(2)}) async-start(), calls=%async_computation | async-start | bytes 1310720 | tf_op jit(solution)/shard_map/all_gather | solution.py:11
  181.1 148.7 %all-gather.62.cloned.1.call-start = ((), (), s32[]{:S(2)}) async-start(), calls=%async_computation.10 | async-start | bytes 4718592 | tf_op jit(solution)/shard_map/all_gather | solution.py:11
  282.7 75.7 %all-gather.64.cloned.1.call-start = ((), (), s32[]{:S(2)}) async-start(), calls=%async_computation.11 | async-start | bytes 1310720 | tf_op jit(solution)/shard_map/all_gather | solution.py:11
  333.0 54.8 %all-gather.44.cloned.1.call-start = ((), (), s32[]{:S(2)}) async-start(), calls=%async_computation.1 | async-start | bytes 1310720 | tf_op jit(solution)/shard_map/all_gather | solution.py:11
  361.2 138.3 %all-gather.66.cloned.1.call-start = ((), (), s32[]{:S(2)}) async-start(), calls=%async_computation.12 | async-start | bytes 4718592 | tf_op jit(solution)/shard_map/all_gather | solution.py:11
  452.5 75.8 %all-gather.68.cloned.1.call-start = ((), (), s32[]{:S(2)}) async-start(), calls=%async_computation.13 | async-start | bytes 1310720 | tf_op jit(solution)/shard_map/all_gather | solution.py:11
  502.8 54.8 %all-gather.46.cloned.1.call-start = ((), (), s32[]{:S(2)}) async-start(), calls=%async_computation.2 | async-start | bytes 1310720 | tf_op jit(solution)/shard_map/all_gather | solution.py:11
  530.9 138.1 %all-gather.70.cloned.1.call-start = ((), (), s32[]{:S(2)}) async-start(), calls=%async_computation.14 | async-start | bytes 4718592 | tf_op jit(solution)/shard_map/all_gather | solution.py:11
  622.0 75.8 %all-gather.72.cloned.1.call-start = ((), (), s32[]{:S(2)}) async-start(), calls=%async_computation.15 | async-start | bytes 1310720 | tf_op jit(solution)/shard_map/all_gather | solution.py:11
  672.3 54.8 %all-gather.48.cloned.1.call-start = ((), (), s32[]{:S(2)}) async-start(), calls=%async_computation.3 | async-start | bytes 1310720 | tf_op jit(solution)/shard_map/all_gather | solution.py:11
  700.4 138.3 %all-gather.74.cloned.1.call-start = ((), (), s32[]{:S(2)}) async-start(), calls=%async_computation.16 | async-start | bytes 4718592 | tf_op jit(solution)/shard_map/all_gather | solution.py:11
  791.7 75.8 %all-gather.76.cloned.1.call-start = ((), (), s32[]{:S(2)}) async-start(), calls=%async_computation.17 | async-start | bytes 1310720 | tf_op jit(solution)/shard_map/all_gather | solution.py:11
  842.0 54.8 %all-gather.50.cloned.1.call-start = ((), (), s32[]{:S(2)}) async-start(), calls=%async_computation.4 | async-start | bytes 1310720 | tf_op jit(solution)/shard_map/all_gather | solution.py:11
  870.2 138.1 %all-gather.78.cloned.1.call-start = ((), (), s32[]{:S(2)}) async-start(), calls=%async_computation.18 | async-start | bytes 4718592 | tf_op jit(solution)/shard_map/all_gather | solution.py:11
  961.3 75.8 %all-gather.80.cloned.1.call-start = ((), (), s32[]{:S(2)}) async-start(), calls=%async_computation.19 | async-start | bytes 1310720 | tf_op jit(solution)/shard_map/all_gather | solution.py:11
  1011.6 54.8 %all-gather.52.cloned.1.call-start = ((), (), s32[]{:S(2)}) async-start(), calls=%async_computation.5 | async-start | bytes 1310720 | tf_op jit(solution)/shard_map/all_gather | solution.py:11
  1039.7 138.1 %all-gather.82.cloned.1.call-start = ((), (), s32[]{:S(2)}) async-start(), calls=%async_computation.20 | async-start | bytes 4718592 | tf_op jit(solution)/shard_map/all_gather | solution.py:11
  1130.8 75.8 %all-gather.84.cloned.1.call-start = ((), (), s32[]{:S(2)}) async-start(), calls=%async_computation.21 | async-start | bytes 1310720 | tf_op jit(solution)/shard_map/all_gather | solution.py:11
  1181.1 54.8 %all-gather.54.cloned.1.call-start = ((), (), s32[]{:S(2)}) async-start(), calls=%async_computation.6 | async-start | bytes 1310720 | tf_op jit(solution)/shard_map/all_gather | solution.py:11
  1209.3 138.2 %all-gather.86.cloned.1.call-start = ((), (), s32[]{:S(2)}) async-start(), calls=%async_computation.22 | async-start | bytes 4718592 | tf_op jit(solution)/shard_map/all_gather | solution.py:11
  1300.4 75.8 %all-gather.88.cloned.1.call-start = ((), (), s32[]{:S(2)}) async-start(), calls=%async_computation.23 | async-start | bytes 1310720 | tf_op jit(solution)/shard_map/all_gather | solution.py:11
  (1 other events, 94.4 us)
Sparse Core Ops, SparseCore 0:
  9.2 29.2 all-gather.55
  102.7 46.8 all-gather.57
  153.0 25.2 all-gather.59
  181.2 26.4 all-gather.41
  282.9 46.8 all-gather.61
  333.1 25.2 all-gather.63
  361.3 26.4 all-gather.43
  452.6 46.8 all-gather.65
  502.9 25.2 all-gather.67
  531.0 26.4 all-gather.45
  622.1 46.8 all-gather.69
  672.4 25.2 all-gather.71
  700.6 26.4 all-gather.47
  791.9 46.8 all-gather.73
  842.2 25.2 all-gather.75
  870.3 26.4 all-gather.49
  961.4 46.8 all-gather.77
  1011.7 25.2 all-gather.79
  1039.8 26.4 all-gather.51
  1130.9 46.8 all-gather.81
  1181.2 25.2 all-gather.83
  1209.4 26.4 all-gather.53
  1300.5 46.8 all-gather.85
  1350.8 25.2 all-gather.87
